TPU v7x, 256 devices: a whole 4x4x8 slice. The times are simulated.
256 devices in a mesh: row: 32 (over z_hi, y, x), col: 8 (over z_lo, core).
Axes of the slice: x: 4, y: 4, z: 8 (z_hi: 2, z_lo: 4; z = z_hi * 4 + z_lo), core: 2. Of those that a mesh axis runs over, the one named last changes fastest.
Arguments:
- deltas: bfloat16 [256, 2, 3584, 512], P(('row', 'col')), may hold values from -192 to 192
- ages: int32 [32, 8], P('row', 'col'), may hold values from 0 to 7
- table: float32 [8], replicated, may hold values from 0.05 to 1
- params: float32 [2, 3584, 512], P(None, ('row', 'col')), may hold values from -6 to 6
- momentum: float32 [2, 3584, 512], P(None, ('row', 'col')), may hold values from -6 to 6
Outputs:
- new_params: float32 [2, 3584, 512], P(None, ('row', 'col'))
- new_momentum: float32 [2, 3584, 512], P(None, ('row', 'col'))
All inputs are finite; a program needn't handle non-finite values.
Results may differ from a plain program's by a relative error of at most 0.0003.
Values sent between devices are 32-bit elements; how exact they have to be, the bound alone decides.
A program may use at most 128 MiB of HBM per device.

v0:
```python
import functools

import jax
import jax.numpy as jnp
from jax import lax
from jax.sharding import Mesh
from jax.sharding import PartitionSpec as P

ROW = ("row_0", "row_1", "row_2")
COL = ("col_0", "col_1")
ROW_COL = ("row_0", "row_1", "row_2", "col_0", "col_1")


momentum_decay = 0.9
outer_rate = 0.7


def one_axis_at_a_time(value, axes):
    return functools.reduce(lax.psum, axes, value)


def local(deltas, ages, table, params, momentum):
    level = jnp.arange(table.shape[0], dtype=jnp.int32)
    weight = jnp.sum(jnp.where(ages.reshape(()) == level, table, jnp.zeros((), table.dtype)))
    total = one_axis_at_a_time(weight, ROW_COL)
    factor = weight / total
    term = deltas[0].astype(jnp.float32) * factor
    summed = lax.psum_scatter(term, ROW_COL, scatter_dimension=1, tiled=True)
    new_momentum = momentum_decay * momentum + summed
    new_params = params - outer_rate * (summed + momentum_decay * new_momentum)
    return (new_params, new_momentum)


def solution(mesh):
    torus = Mesh(mesh.devices.reshape(2, 4, 4, 4, 2), ("row_0", "row_1", "row_2", "col_0", "col_1"))
    in_specs = (
        P(ROW_COL, None, None, None),
        P(ROW, COL),
        P(),
        P(None, ROW_COL, None),
        P(None, ROW_COL, None),
    )
    out_specs = (P(None, ROW_COL, None), P(None, ROW_COL, None))
    return jax.shard_map(local, mesh=torus, in_specs=in_specs, out_specs=out_specs, check_vma=False)
```

profile of v0, /device:TPU:1, one launch (start us, length us, event | category | flops | bytes accessed | tf_op | source)
XLA Modules:
  0.0 391.4 jit_solution(4721865014794327608)
XLA Ops:
  7.2 0.0 all-reduce.3.cloned.1.call-start
  7.9 1.3 fusion
  9.1 10.6 %psum.35 = f32[]{:T(128)} all-reduce(f32[]{:T(128)} %fusion), channel_id=1, replica_groups=mesh['row_0'=2,'row_1'=4,'row_2'=4,'col_0'=4,'col_1'=2] {'row_0'}, use_global_device_ids=true, to_apply=%region_1.2 | all-reduce | flops 1 | bytes 8 | tf_op jit(solution)/shard_map/psum | solution.py:19
  19.8 9.3 %psum.36 = f32[]{:T(128)} all-reduce(f32[]{:T(128)} %psum.35), channel_id=1, replica_groups=mesh['row_0'=2,'row_1'=4,'row_2'=4,'col_0'=4,'col_1'=2] {'row_1'}, use_global_device_ids=true, to_apply=%region_2.3 | all-reduce | flops 1 | bytes 8 | tf_op jit(solution)/shard_map/psum | solution.py:19
  29.1 9.1 %psum.37 = f32[]{:T(128)} all-reduce(f32[]{:T(128)} %psum.36), channel_id=1, replica_groups=mesh['row_0'=2,'row_1'=4,'row_2'=4,'col_0'=4,'col_1'=2] {'row_2'}, use_global_device_ids=true, to_apply=%region_3.4 | all-reduce | flops 1 | bytes 8 | tf_op jit(solution)/shard_map/psum | solution.py:19
  38.2 10.0 %psum.38 = f32[]{:T(128)} all-reduce(f32[]{:T(128)} %psum.37), channel_id=1, replica_groups=mesh['row_0'=2,'row_1'=4,'row_2'=4,'col_0'=4,'col_1'=2] {'col_0'}, use_global_device_ids=true, to_apply=%region_4.5 | all-reduce | flops 1 | bytes 8 | tf_op jit(solution)/shard_map/psum | solution.py:19
  48.2 10.6 %psum.39 = f32[]{:T(128)} all-reduce(f32[]{:T(128)} %psum.38), channel_id=1, replica_groups=mesh['row_0'=2,'row_1'=4,'row_2'=4,'col_0'=4,'col_1'=2] {'col_1'}, use_global_device_ids=true, to_apply=%region_5.6 | all-reduce | flops 1 | bytes 8 | tf_op jit(solution)/shard_map/psum | solution.py:19
  60.2 10.4 %multiply_bitcast_fusion = f32[2,3584,512]{2,1,0:T(8,128)} fusion(bf16[1,2,3584,512]{3,2,1,0:T(8,128)(2,1)} %param.5, f32[]{:T(128)S(6)} %div.3), kind=kLoop, calls=%fused_computation | loop fusion | flops 7340032 | bytes 22020100 | tf_op jit(solution)/shard_map/mul | solution.py:27
  70.6 25.3 %copy.9 = f32[2,3584,512]{2,0,1:T(2,128)} copy(f32[2,3584,512]{2,1,0:T(8,128)} %multiply_bitcast_fusion) | data formatting | bytes 29360128 | tf_op jit(solution)/shard_map/mul | solution.py:27
  95.8 0.0 copy-start
  95.8 0.0 copy-start.1
  95.8 0.0 all-reduce.3.cloned.1.call-update
  95.9 287.1 %all-reduce.3.cloned.1.call-done = f32[2,3584,512]{2,0,1:T(2,128)} async-done(((f32[2,3584,512]{2,0,1:T(2,128)}), f32[2,3584,512]{2,0,1:T(2,128)}) %all-reduce.3.cloned.1.call-update) | async-done | bytes 14680080
  383.0 0.0 copy-done
  383.0 0.0 copy-done.1
  383.0 1.5 multiply_subtract_fusion
Async XLA Ops:
  7.2 375.8 %all-reduce.3.cloned.1.call-start = ((), (), s32[]{:S(2)}) async-start(), calls=%async_computation | async-start | bytes 29360128
  95.8 287.1 %copy-start = (f32[2,14,512]{2,0,1:T(2,128)S(1)}, f32[2,14,512]{2,0,1:T(2,128)}, u32[]{:S(2)}) copy-start(f32[2,14,512]{2,0,1:T(2,128)} %param.8) | copy-start | bytes 172036
  95.8 287.1 %copy-start.1 = (f32[2,14,512]{2,0,1:T(2,128)S(1)}, f32[2,14,512]{2,0,1:T(2,128)}, u32[]{:S(2)}) copy-start(f32[2,14,512]{2,0,1:T(2,128)} %param.9) | copy-start | bytes 172036
Sparse Core Ops, SparseCore 0:
  96.0 286.9 all-reduce.2
where the time goes:
time: 392 us; the launch traced here: 391 us
  waiting for transfers between devices  287 us (73%)
  blocking collectives  49.7 us (13%)
  local copies, waits for them, and re-layouts  25.3 us (6%)
  between operations  16 us (4%)
  other arithmetic  13.2 us (3%)
    unnamed x2, waiting for transfers between devices  287 us
    psum x5, blocking collectives, one_axis_at_a_time(): return functools.reduce(lax.psum, axes, value)  49.7 us
    mul x1, local copies, waits for them, and re-layouts, local(): term = deltas[0].astype(jnp.float32) * factor  25.3 us
    mul x1, other arithmetic, local(): term = deltas[0].astype(jnp.float32) * factor  10.4 us
  transfers between devices with their start and end apart: 1, of which 1 were waited for; matrix products, arithmetic and copies ran while one was open for 0% of the time, Pallas kernels for 0%

commit v1 on v0

v1 whole, which is shorter than its diff:
```python
import functools

import jax
import jax.numpy as jnp
from jax import lax
from jax.experimental import pallas as pl
from jax.experimental.pallas import tpu as pltpu
from jax.sharding import Mesh
from jax.sharding import PartitionSpec as P

ROW = ("z_hi", "y", "x")
COL = ("z_lo", "core")
ROW_COL = ROW + COL
MESH = pl.DeviceIdType.MESH
F32 = jnp.float32

momentum_decay = 0.9
outer_rate = 0.7

BLOCK = 112
WIN = 32
N_SEM = 160
A, B, C, D = range(4)


def kernel(delta, ages, table, out, theirs, ours, give, got, mine, t1, t2, tc, u2, zr,
           g1, g1c, g2, g2c, fin, wt, wx, send_sems, recv_sems, load_sems):
    zh, y, x, zl, core = [lax.axis_index(name) for name in ROW_COL]
    z = zh * 4 + zl
    barrier = pltpu.get_barrier_semaphore()

    load_theirs = pltpu.make_async_copy(delta.at[0, 1 - core], theirs, load_sems.at[0])
    load_ours = pltpu.make_async_copy(delta.at[0, core], ours, load_sems.at[1])
    load_theirs.start()
    load_ours.start()

    def at_z(there):
        there = lax.rem(there + 16, 8)
        return (there // 4, y, x, lax.rem(there, 4), core)

    def at_axis(is_x, step):
        return (zh, lax.rem(y + (1 - is_x) * step + 4, 4), lax.rem(x + is_x * step + 4, 4), zl, core)

    partner = (zh, y, x, zl, 1 - core)
    peers = [partner]
    peers += [at_axis(1, s) for s in (1, 2, 3)] + [at_axis(0, s) for s in (1, 2, 3)]
    peers += [at_z(z + s) for s in range(1, 8)]
    for peer in peers:
        pl.semaphore_signal(barrier, inc=1, device_id=peer, device_id_type=MESH)

    weight = table[ages[0, 0]]
    wt[0] = jnp.full((8, 128), weight, F32)

    sent = []

    def send(src, dst, device):
        i = len(sent)
        copy = pltpu.make_async_remote_copy(
            src_ref=src, dst_ref=dst, send_sem=send_sems.at[i], recv_sem=recv_sems.at[i],
            device_id=device, device_id_type=MESH)
        copy.start()
        sent.append(copy)
        return copy

    first = {A: 1, B: 0, C: 1 - core, D: 1 - core}
    first_of_partner = {A: 1, B: 0, C: core, D: core}

    def along(is_x):
        return is_x * x + (1 - is_x) * y

    def across(is_x):
        return is_x * y + (1 - is_x) * x

    def wrap4(value):
        return lax.rem(value + 4, 4)

    def block_of(unit, is_x, slot):
        if unit == C:
            half, d, j = slot // 16, lax.rem(slot, 16) // 4, lax.rem(slot, 4)
        else:
            d, half, j = slot // 8, lax.rem(slot, 8) // 4, lax.rem(slot, 4)
        return half * 16 + j * (4 * is_x + (1 - is_x)) + d * (is_x + 4 * (1 - is_x))

    def term(src, unit, is_x, slot):
        start = pl.multiple_of(block_of(unit, is_x, slot) * BLOCK, 16)
        return src[pl.ds(start, BLOCK), unit * 128:(unit + 1) * 128].astype(F32) * weight

    def chunk(unit, is_x, step):
        if unit == C:
            return lax.rem(zh + step, 2) * 16, 16
        return wrap4(along(is_x) + step) * 8, 8

    order = [(A, 2), (B, 2), (C, 1), (A, 1), (A, -1), (B, 1), (B, -1), (C, 0),
             (D, 2), (D, 1), (D, -1), (A, 0), (B, 0), (D, 0)]

    load_theirs.wait()
    swaps = {}
    for n, (unit, step) in enumerate(order):
        is_x = first_of_partner[unit]
        base, count = chunk(unit, is_x, step)

        @pl.loop(0, count)
        def _(k):
            give[unit, base + k] = term(theirs, unit, is_x, base + k)

        if n == 0:
            pl.semaphore_wait(barrier, len(peers))
        swaps[unit, step] = send(give.at[unit, pl.ds(base, count)], got.at[unit, pl.ds(base, count)], partner)
    swap_weight = send(wt.at[0], wt.at[1], partner)
    load_ours.wait()

    def settle(unit, step):
        is_x = first[unit]
        base, count = chunk(unit, is_x, step)
        swaps[unit, step].wait_recv()

        @pl.loop(0, count)
        def _(k):
            mine[unit, base + k] = got[unit, base + k] + term(ours, unit, is_x, base + k)

    class Tree:
        def __init__(self, piece, slots, is_x, me):
            self.piece, self.slots, self.is_x, self.me = piece, slots, is_x, me
            self.m0, self.m1, self.m2 = {}, {}, {}

        def far(self):
            for s in (1, -1):
                src = self.piece(s < 0, wrap4(self.me + 2))
                self.m0[s] = send(src, self.slots.at[0, int(s < 0)], at_axis(self.is_x, s))

        def near(self):
            for s in (1, -1):
                src = self.piece(s > 0, wrap4(self.me + s))
                self.m1[s] = send(src, self.slots.at[1, int(s < 0)], at_axis(self.is_x, s))

        def relay(self):
            for s in (1, -1):
                self.m0[s].wait_recv()
                held = self.slots.at[0, int(s < 0)]
                held[...] = held[...] + self.piece(s < 0, wrap4(self.me + s))[...]
                self.m2[s] = send(held, self.slots.at[2, int(s < 0)], at_axis(self.is_x, s))

        def finish(self, put):
            for s in (1, -1):
                self.m1[s].wait_recv()
                self.m2[s].wait_recv()
            for h in (0, 1):
                put(h, self.piece(h, self.me)[...] + self.slots[2, h] + self.slots[1, 1 - h])

    def first_tree(n, unit):
        is_x = first[unit]
        return Tree(lambda h, d: mine.at[unit, pl.ds(d * 8 + int(h) * 4, 4)], t1.at[n], is_x, along(is_x))

    def second_tree(n, unit):
        is_x = first[unit]
        return Tree(lambda h, d: g1.at[n, int(h), d], t2.at[n], 1 - is_x, across(is_x))

    trees1 = {unit: first_tree(n, unit) for n, unit in enumerate((A, B, D))}
    trees2 = {unit: second_tree(n, unit) for n, unit in enumerate((A, B, D))}
    place = {A: 0, B: 1, D: 2}

    def end_first(unit):
        def put(h, value):
            g1[place[unit], h] = value
        trees1[unit].finish(put)

    def end_second(unit):
        def put(h, value):
            g2[place[unit], h] = value
        trees2[unit].finish(put)

    dist = (4, 3, 3, 2, 2, 1, 1)

    def window(there):
        there = lax.rem(there + 16, 8)
        low = lax.rem(there, 4)
        return there // 4, pl.multiple_of((low // 2) * 56 + lax.rem(low, 2) * 24, 8)

    def c_piece(there, half):
        up, start = window(there)
        return mine.at[C, pl.ds(up * 16 + half * 8, 8), pl.ds(start, WIN)]

    def c_half(s, i):
        return int(s < 0) if i % 2 == 0 else int(s > 0)

    c_sent = {}

    def c_step(i):
        for s in (1, -1):
            n = int(s < 0)
            piece = c_piece(z + s * dist[i], c_half(s, i))
            if i >= 2:
                c_sent[s, i - 2].wait_recv()
                held = tc.at[n, i - 2]
                held[...] = held[...] + piece[...]
                piece = held
            c_sent[s, i] = send(piece, tc.at[n, i], at_z(z + s))

    def c_finish():
        for i in (5, 6):
            for s in (1, -1):
                c_sent[s, i].wait_recv()
        for half in (0, 1):
            g1c[half * 8:half * 8 + 8] = c_piece(z, half)[...] + tc[half, 6] + tc[1 - half, 5]

    c_x = first[C]
    tree_c = Tree(lambda h, d: g1c.at[pl.ds(d * 4 + int(h) * 2, 2)], u2, c_x, along(c_x))
    c_last = []

    def c_second_end():
        def put(h, value):
            g2c[h * 2:h * 2 + 2] = value
        tree_c.finish(put)
        for s in (2, 1, 3):
            c_last.append(send(g2c.at[wrap4(across(c_x) + s)], g2c.at[3 + s], at_axis(1 - c_x, s)))

    def c_end():
        for copy in c_last:
            copy.wait_recv()
        fin[core, C] = g2c[across(c_x)] + (g2c[4] + g2c[5] + g2c[6])

    class Ring:
        def __init__(self, low, count):
            self.low, self.count = low, count
            self.up, self.down = [], []

        def piece(self, there):
            half, start = window(there)
            return g2.at[pl.ds(self.low, self.count), half, pl.ds(start, WIN)]

        def slot(self, i):
            return zr.at[i, pl.ds(self.low, self.count)]

        def step(self, i):
            for s, far, copies, base in ((1, 4, self.up, 0), (-1, 3, self.down, 4)):
                if i >= far:
                    continue
                piece = self.piece(z + s * (far - i))
                if i:
                    copies[i - 1].wait_recv()
                    held = self.slot(base + i - 1)
                    held[...] = held[...] + piece[...]
                    piece = held
                copies.append(send(piece, self.slot(base + i), at_z(z + s)))

        def end(self, units):
            self.up[3].wait_recv()
            self.down[2].wait_recv()
            total = self.piece(z)[...] + self.slot(3)[...] + self.slot(6)[...]
            for n, unit in enumerate(units):
                fin[core, unit] = total[n]

    ring_ab, ring_d = Ring(0, 2), Ring(2, 1)

    weight_sent = []

    def weights(stage):
        spans = ((), (1, 2, 3), (1, 2, 3), tuple(range(1, 8)))
        if stage == 0:
            swap_weight.wait_recv()
            wt[2] = wt[0] + wt[1]
        else:
            for copy in weight_sent:
                copy.wait_recv()
            weight_sent.clear()
            value = wt[1 + stage]
            low = (0, 3, 6)[stage - 1]
            for n in range(len(spans[stage])):
                value = value + wx[low + n]
            wt[2 + stage] = value
        if stage < 3:
            low = (0, 3, 6)[stage]
            for n, s in enumerate(spans[stage + 1]):
                device = at_z(z + s) if stage == 2 else at_axis(1 - stage, s)
                weight_sent.append(send(wt.at[2 + stage], wx.at[low + n], device))

    settle(A, 2)
    trees1[A].far()
    settle(B, 2)
    trees1[B].far()
    settle(C, 1)
    c_step(0)
    settle(A, 1)
    settle(A, -1)
    trees1[A].near()
    settle(B, 1)
    settle(B, -1)
    trees1[B].near()
    settle(C, 0)
    c_step(1)
    weights(0)
    c_step(2)
    trees1[A].relay()
    trees1[B].relay()
    settle(D, 2)
    trees1[D].far()
    settle(D, 1)
    settle(D, -1)
    trees1[D].near()
    weights(1)
    c_step(3)
    settle(A, 0)
    settle(B, 0)
    settle(D, 0)
    c_step(4)
    weights(2)
    c_step(5)
    c_step(6)
    for unit in (A, B):
        end_first(unit)
        trees2[unit].far()
        trees2[unit].near()
    trees1[D].relay()
    trees2[A].relay()
    trees2[B].relay()
    c_finish()
    tree_c.far()
    tree_c.near()
    end_second(A)
    end_second(B)
    ring_ab.step(0)
    tree_c.relay()
    ring_ab.step(1)
    end_first(D)
    trees2[D].far()
    trees2[D].near()
    c_second_end()
    ring_ab.step(2)
    trees2[D].relay()
    ring_ab.step(3)
    end_second(D)
    ring_d.step(0)
    ring_ab.end((A, B))
    ring_d.step(1)
    c_end()
    weights(3)
    early = len(sent) - 4
    ring_d.step(2)
    for copy in sent[:early]:
        copy.wait_send()
    ring_d.step(3)
    ring_d.end((D,))
    last = send(fin.at[core], fin.at[core], partner)
    last.wait_recv()
    total = wt[5]
    for odd in (0, 1):
        for c in (0, 1):
            @pl.when((lax.rem(zl, 2) == odd) & (core == c))
            def _():
                low = 4 * odd + 14 * c
                for p in (0, 1):
                    for unit in range(4):
                        out[p, :, unit * 128:(unit + 1) * 128] = fin[p, unit, low:low + 14] / total[:1]
    for copy in sent[early:]:
        copy.wait_send()
    assert len(sent) <= N_SEM


def merge(deltas, ages, table):
    vmem = lambda *shape: pltpu.VMEM(shape, F32)
    return pl.pallas_call(
        kernel,
        out_shape=jax.ShapeDtypeStruct((2, 14, 512), F32),
        in_specs=[
            pl.BlockSpec(memory_space=pl.ANY),
            pl.BlockSpec(memory_space=pltpu.SMEM),
            pl.BlockSpec(memory_space=pltpu.SMEM),
        ],
        out_specs=pl.BlockSpec(memory_space=pltpu.VMEM),
        scratch_shapes=[
            pltpu.VMEM((3584, 512), jnp.bfloat16),
            pltpu.VMEM((3584, 512), jnp.bfloat16),
            vmem(4, 32, BLOCK, 128),
            vmem(4, 32, BLOCK, 128),
            vmem(4, 32, BLOCK, 128),
            vmem(3, 3, 2, 4, BLOCK, 128),
            vmem(3, 3, 2, BLOCK, 128),
            vmem(2, 7, 8, WIN, 128),
            vmem(3, 2, 2, WIN, 128),
            vmem(7, 3, WIN, 128),
            vmem(3, 2, 4, BLOCK, 128),
            vmem(16, WIN, 128),
            vmem(3, 2, BLOCK, 128),
            vmem(7, WIN, 128),
            vmem(2, 4, WIN, 128),
            vmem(6, 8, 128),
            vmem(13, 8, 128),
            pltpu.SemaphoreType.DMA((N_SEM,)),
            pltpu.SemaphoreType.DMA((N_SEM,)),
            pltpu.SemaphoreType.DMA((2,)),
        ],
        compiler_params=pltpu.CompilerParams(
            collective_id=0, has_side_effects=True, vmem_limit_bytes=60 * 2**20),
        name="merge",
    )(deltas, ages, table)


def local(deltas, ages, table, params, momentum):
    merged = merge(deltas, ages, table)
    new_momentum = momentum_decay * momentum + merged
    new_params = params - outer_rate * (merged + momentum_decay * new_momentum)
    return (new_params, new_momentum)


def solution(mesh):
    torus = Mesh(mesh.devices.reshape(2, 4, 4, 4, 2), ROW_COL)
    in_specs = (
        P(ROW_COL, None, None, None),
        P(ROW, COL),
        P(),
        P(None, ROW_COL, None),
        P(None, ROW_COL, None),
    )
    out_specs = (P(None, ROW_COL, None), P(None, ROW_COL, None))
    return jax.shard_map(local, mesh=torus, in_specs=in_specs, out_specs=out_specs, check_vma=False)
```

time: 392 us -> 73.8 us (0.19)
  waiting for transfers between devices: 287 us -> 0 us
  Pallas kernels: 0 us -> 70 us
  blocking collectives: 49.7 us -> 0 us
  local copies, waits for them, and re-layouts: 25.3 us -> 1.34 us
  between operations: 16 us -> 1.34 us
  other arithmetic: 13.2 us -> 0.88 us
    unnamed x2 -> x0, waiting for transfers between devices: 287 us -> none
    pallas_call x0 -> x1, Pallas kernels: none -> 70 us  [merge(): pl.pallas_call(kernel, out_shape=jax.ShapeDtypeStruct((2, 14, 512), F32),...]
    psum x5 -> x0, blocking collectives: 49.7 us -> none  [one_axis_at_a_time(): return functools.reduce(lax.psum, axes, value)]
    mul x1 -> x0, local copies, waits for them, and re-layouts: 25.3 us -> none  [local(): term = deltas[0].astype(jnp.float32) * factor]
    mul x1 -> x0, other arithmetic: 10.4 us -> none  [local(): term = deltas[0].astype(jnp.float32) * factor]
  transfers between devices with their start and end apart: 1 -> 0, of which waited for: 1 -> 0; matrix products, arithmetic and copies ran while one was open for 0% -> 0% of each run, Pallas kernels for 0% -> 0%
where the time goes in v1:
time: 73.8 us; the launch traced here: 73.6 us
  Pallas kernels  70 us (95%)
  local copies, waits for them, and re-layouts  1.34 us (2%)
  between operations  1.34 us (2%)
  other arithmetic  0.88 us (1%)
    pallas_call x1, Pallas kernels, merge(): pl.pallas_call(kernel, out_shape=jax.ShapeDtypeStruct((2, 14, 512), F32),...  70 us

profile of v1, /device:TPU:1, one launch (start us, length us, event | category | flops | bytes accessed | tf_op | source)
XLA Modules:
  0.0 73.6 jit_solution(14692157152024508920)
XLA Ops:
  0.6 0.0 copy-start
  0.6 0.0 copy-start.1
  1.3 70.0 %merge.1 = f32[2,14,512]{2,1,0:T(8,128)} custom-call(bf16[1,2,3584,512]{3,2,1,0:T(8,128)(2,1)} %delta.1, s32[1,1]{1,0:T(1,128)S(6)} %copy.17.ages, f32[8]{0:T(128)} %table.1), custom_call_target="tpu_custom_call" | custom-call | tf_op jit(solution)/shard_map/merge/pallas_call | solution.py:361
  71.3 0.0 copy-done
  71.4 0.0 copy-done.1
  71.4 0.9 %fusion = (f32[2,14,512]{2,1,0:T(8,128)S(1)}, f32[2,14,512]{2,1,0:T(8,128)S(1)}) fusion(f32[2,14,512]{2,1,0:T(8,128)} %merge.1, f32[2,14,512]{2,0,1:T(2,128)S(1)} %copy-done, f32[2,14,512]{2,0,1:T(2,128)S(1)} %copy-done.1), kind=kLoop, calls=%fused_computation.2 | loop fusion | flops 86016 | bytes 286720 | tf_op jit(solution)/shard_map/add | solution.py:400
  72.2 0.7 copy.10
  72.9 0.7 copy.9
Async XLA Ops:
  0.6 70.7 %copy-start = (f32[2,14,512]{2,0,1:T(2,128)S(1)}, f32[2,14,512]{2,0,1:T(2,128)}, u32[]{:S(2)}) copy-start(f32[2,14,512]{2,0,1:T(2,128)} %param.9) | copy-start | bytes 172036
  0.6 70.7 %copy-start.1 = (f32[2,14,512]{2,0,1:T(2,128)S(1)}, f32[2,14,512]{2,0,1:T(2,128)}, u32[]{:S(2)}) copy-start(f32[2,14,512]{2,0,1:T(2,128)} %param.8) | copy-start | bytes 172036

commit v2 on v0

v2 whole, which is shorter than its diff:
```python
import jax
import jax.numpy as jnp
from jax import lax
from jax.experimental import pallas as pl
from jax.experimental.pallas import tpu as pltpu
from jax.sharding import Mesh
from jax.sharding import PartitionSpec as P

ROW = ("z_hi", "y", "x")
COL = ("z_lo", "core")
ROW_COL = ROW + COL
MESH = pl.DeviceIdType.MESH
F32 = jnp.float32

momentum_decay = 0.9
outer_rate = 0.7

BLOCK = 112
WIN = 32
N_SEND, N_RECV = 13, 55
X, Y, ZX, ZY = "X", "Y", "ZX", "ZY"
KINDS = ((X, Y, ZX, ZY), (X, Y, X, Y))

ORDERS = (
    ((2, 1, 0), (0, 2), (2, 1, 1), (1, 2), (3, 1, 0), (3, 1, 1), (2, 0, 0), (2, 0, 1),
     (0, 1), (0, -1), (3, 0, 0), (3, 0, 1), (1, 1), (1, -1), (0, 0), (1, 0)),
    ((0, 2), (1, 2), (0, 1), (0, -1), (1, 1), (1, -1), (2, 2), (3, 2),
     (2, 1), (2, -1), (3, 1), (3, -1), (0, 0), (1, 0), (2, 0), (3, 0)),
)
AHEAD = 4


def wrap4(value):
    return lax.rem(value + 4, 4)


def kernel(delta, ages, table, out, age, levels, theirs, ours, give, got, mine, t1, t2, tc, u2, zr,
           g1, g1c, g2, g2c, fin, wt, wx, send_sems, recv_sems, swap_send, swap_recv, load_sems):
    zh, y, x, zl, core = [lax.axis_index(name) for name in ROW_COL]
    z = zh * 4 + zl
    barrier = pltpu.get_barrier_semaphore()

    load_age = pltpu.make_async_copy(ages, age, load_sems.at[5])
    load_levels = pltpu.make_async_copy(table, levels, load_sems.at[6])
    load_age.start()
    load_levels.start()

    def program(me):
        kinds, other_kinds = KINDS[me], KINDS[1 - me]
        order, other_order = ORDERS[me], ORDERS[1 - me]

        def load(source, target, unit, sem):
            lanes = pl.ds(unit * 128, 128)
            return pltpu.make_async_copy(delta.at[0, source, :, lanes], target.at[:, lanes], load_sems.at[sem])

        first_use = list(dict.fromkeys(unit for unit, *_ in other_order))
        load_theirs = {unit: load(1 - me, theirs, unit, unit) for unit in first_use}
        load_ours = pltpu.make_async_copy(delta.at[0, me], ours, load_sems.at[4])
        for unit in first_use:
            load_theirs[unit].start()

        def at_z(there):
            there = lax.rem(there + 16, 8)
            return (there // 4, y, x, lax.rem(there, 4), me)

        def at_axis(axis, step):
            if axis == X:
                return (zh, y, wrap4(x + step), zl, me)
            return (zh, wrap4(y + step), x, zl, me)

        partner = (zh, y, x, zl, 1 - me)
        peers = [partner]
        peers += [at_axis(axis, s) for axis in (X, Y) for s in (1, 2, 3)]
        peers += [at_z(z + s) for s in range(1, 8)]
        for peer in peers:
            pl.semaphore_signal(barrier, inc=1, device_id=peer, device_id_type=MESH)
        load_age.wait()
        load_levels.wait()
        weight = levels[age[0, 0]]
        wt[0] = jnp.full((8, 128), weight, F32)

        def copy_to(device, src, dst, send_sem, recv_sem):
            return pltpu.make_async_remote_copy(
                src_ref=src, dst_ref=dst, send_sem=send_sem, recv_sem=recv_sem,
                device_id=device, device_id_type=MESH)

        groups, recvs = [], []

        def new_recv():
            recvs.append(len(recvs))
            return recv_sems.at[recvs[-1]]

        class Group:
            def __init__(self, whole):
                self.whole, self.send_sem = whole, send_sems.at[len(groups)]
                groups.append(self)

            def send(self, src, dst, device, recv_sem):
                copy = copy_to(device, src, dst, self.send_sem, recv_sem)
                copy.start()
                return copy

            def drain(self):
                copy_to(partner, self.whole, self.whole, self.send_sem, recv_sems.at[0]).wait_send()

        def arrived(whole, recv_sem):
            copy_to(partner, whole, whole, send_sems.at[0], recv_sem).wait_recv()

        def swap(src, dst, i):
            return copy_to(partner, src, dst, swap_send.at[max(i - 15, 0)], swap_recv.at[i])

        def position(axis):
            return x if axis == X else y

        def cross(axis):
            return Y if axis == X else X

        def term(src, unit, kind, slot):
            if kind in (ZX, ZY):
                half, d, j = slot // 16, lax.rem(slot, 16) // 4, lax.rem(slot, 4)
            else:
                d, half, j = slot // 8, lax.rem(slot, 8) // 4, lax.rem(slot, 4)
            block = half * 16 + (j * 4 + d if kind in (X, ZX) else d * 4 + j)
            start = pl.multiple_of(block * BLOCK, 16)
            return src[pl.ds(start, BLOCK), unit * 128:(unit + 1) * 128].astype(F32) * weight

        def chunk(kind, step):
            if kind in (ZX, ZY):
                return lax.rem(zh + step[0], 2) * 16 + 8 * step[1]
            return wrap4(position(kind) + step[0]) * 8

        gifts = []

        def put_together(n):
            unit, *step = other_order[n]
            kind = other_kinds[unit]
            if unit in load_theirs:
                load_theirs.pop(unit).wait()
            base = chunk(kind, step)

            @pl.loop(0, 8)
            def _(k):
                give[unit, base + k] = term(theirs, unit, kind, base + k)

            gifts.append(swap(give.at[unit, pl.ds(base, 8)], got.at[unit, pl.ds(base, 8)], n))

        def settle(n):
            unit, *step = order[n]
            kind = kinds[unit]
            base = chunk(kind, step)
            swap(got.at[unit, pl.ds(base, 8)], got.at[unit, pl.ds(base, 8)], n).wait_recv()

            @pl.loop(0, 8)
            def _(k):
                mine[unit, base + k] = got[unit, base + k] + term(ours, unit, kind, base + k)

            if n + AHEAD < 16:
                put_together(n + AHEAD)
                gifts[-1].start()

        class Tree:
            def __init__(self, piece, slots, axis):
                self.piece, self.slots, self.axis, self.at = piece, slots, axis, position(axis)
                self.group = Group(slots)
                self.m0, self.first, self.rest = {}, {1: new_recv(), -1: new_recv()}, new_recv()

            def far(self):
                for s in (1, -1):
                    src = self.piece(int(s < 0), wrap4(self.at + 2))
                    dst = self.slots.at[0, int(s < 0)]
                    self.m0[s] = self.group.send(src, dst, at_axis(self.axis, s), self.first[s])

            def near(self):
                for s in (1, -1):
                    src = self.piece(int(s > 0), wrap4(self.at + s))
                    self.group.send(src, self.slots.at[1, int(s < 0)], at_axis(self.axis, s), self.rest)

            def relay(self):
                for s in (1, -1):
                    self.m0[s].wait_recv()
                    held = self.slots.at[0, int(s < 0)]
                    held[...] = held[...] + self.piece(int(s < 0), wrap4(self.at + s))[...]
                    self.group.send(held, self.slots.at[2, int(s < 0)], at_axis(self.axis, s), self.rest)

            def finish(self, put):
                arrived(self.slots.at[pl.ds(1, 2)], self.rest)
                for h in (0, 1):
                    put(h, self.piece(h, self.at)[...] + self.slots[2, h] + self.slots[1, 1 - h])

        def window(there):
            there = lax.rem(there + 16, 8)
            low = lax.rem(there, 4)
            return there // 4, pl.multiple_of((low // 2) * 56 + lax.rem(low, 2) * 24, 8)

        class Flat:
            def __init__(self, unit):
                axis = kinds[unit]
                self.unit = unit
                self.one = Tree(lambda h, d: mine.at[unit, pl.ds(d * 8 + h * 4, 4)], t1.at[unit], axis)
                self.two = Tree(lambda h, d: g1.at[unit, h, d], t2.at[unit], cross(axis))
                self.group, self.last, self.far_sem = Group(zr.at[unit]), new_recv(), new_recv()
                self.way = 1 if unit % 2 == 0 else -1

            def end_one(self):
                def put(h, value):
                    g1[self.unit, h] = value
                self.one.finish(put)
                self.two.far()
                self.two.near()

            def end_two(self):
                def put(h, value):
                    g2[self.unit, h] = value
                self.two.finish(put)
                self.send_z(4, 2 * self.way, 4, self.far_sem)
                for s in (1, -1):
                    self.send_z(3 * s, s, 5 + int(s < 0), self.far_sem)
                for s in (1, -1):
                    self.send_z(s, s, int(s < 0), self.last)

            def piece_z(self, there):
                half, start = window(there)
                return g2.at[self.unit, half, pl.ds(start, WIN)]

            def send_z(self, there, step, slot, sem):
                self.group.send(self.piece_z(z + there), zr.at[self.unit, slot], at_z(z + step), sem)

            def relay_z(self):
                arrived(zr.at[self.unit, pl.ds(4, 3)], self.far_sem)
                for s in (1, -1):
                    held = zr.at[self.unit, 5 + int(s < 0)]
                    value = held[...] + self.piece_z(z + 2 * s)[...]
                    if s == self.way:
                        value = value + zr[self.unit, 4]
                    held[...] = value
                    self.group.send(held, zr.at[self.unit, 2 + int(s < 0)], at_z(z + 2 * s), self.last)

            def end(self):
                arrived(zr.at[self.unit, pl.ds(0, 4)], self.last)
                value = self.piece_z(z)[...]
                for n in range(4):
                    value = value + zr[self.unit, n]
                fin[me, self.unit] = value

        class Deep:
            dist = (4, 3, 3, 2, 2, 1, 1)

            def __init__(self, unit):
                self.unit, self.n = unit, unit - 2
                self.axis = X if kinds[unit] == ZX else Y
                self.copies, self.ring = {}, Group(tc.at[self.n])
                self.two = Tree(lambda h, d: g1c.at[self.n, pl.ds(d * 4 + h * 2, 2)], u2.at[self.n], self.axis)
                self.group, self.last = Group(g2c.at[self.n, pl.ds(4, 3)]), new_recv()

            def piece(self, there, half):
                up, start = window(there)
                return mine.at[self.unit, pl.ds(up * 16 + half * 8, 8), pl.ds(start, WIN)]

            def step(self, i, ways=(1, -1)):
                for s in ways:
                    k = int(s < 0)
                    piece = self.piece(z + s * self.dist[i], k if i % 2 == 0 else 1 - k)
                    if i >= 2:
                        self.copies[s, i - 2].wait_recv()
                        held = tc.at[self.n, k, i - 2]
                        held[...] = held[...] + piece[...]
                        piece = held
                    self.copies[s, i] = self.ring.send(piece, tc.at[self.n, k, i], at_z(z + s), new_recv())

            def end_one(self):
                for i in (5, 6):
                    for s in (1, -1):
                        self.copies[s, i].wait_recv()
                for half in (0, 1):
                    g1c[self.n, half * 8:half * 8 + 8] = (
                        self.piece(z, half)[...] + tc[self.n, half, 6] + tc[self.n, 1 - half, 5])
                self.two.far()
                self.two.near()

            def end_two(self):
                def put(h, value):
                    g2c[self.n, h * 2:h * 2 + 2] = value
                self.two.finish(put)
                axis = cross(self.axis)
                for s in (2, 1, 3):
                    src = g2c.at[self.n, wrap4(position(axis) + s)]
                    self.group.send(src, g2c.at[self.n, 3 + s], at_axis(axis, s), self.last)

            def end(self):
                arrived(g2c.at[self.n, pl.ds(4, 3)], self.last)
                fin[me, self.unit] = g2c[self.n, position(cross(self.axis))] + (
                    g2c[self.n, 4] + g2c[self.n, 5] + g2c[self.n, 6])

        weight_group, weight_sems = Group(wx), [new_recv() for _ in range(3)]

        def weights(stage):
            spans = ((), (1, 2, 3), (1, 2, 3), (4, 3, 5, 2, 6, 1, 7))
            lows = (0, 3, 6)
            if stage == 0:
                swap(wt.at[1], wt.at[1], 16).wait_recv()
                wt[2] = wt[0] + wt[1]
            else:
                low, count = lows[stage - 1], len(spans[stage])
                arrived(wx.at[pl.ds(low, count)], weight_sems[stage - 1])
                value = wt[1 + stage]
                for n in range(count):
                    value = value + wx[low + n]
                wt[2 + stage] = value
            if stage < 3:
                for n, s in enumerate(spans[stage + 1]):
                    device = at_z(z + s) if stage == 2 else at_axis((X, Y)[stage], s)
                    weight_group.send(wt.at[2 + stage], wx.at[lows[stage] + n], device, weight_sems[stage])

        put_together(0)
        load_ours.start()
        pl.semaphore_wait(barrier, len(peers))
        swap_weight = swap(wt.at[0], wt.at[1], 16)
        swap_weight.start()
        gifts[0].start()
        for n in range(1, AHEAD):
            put_together(n)
            gifts[n].start()
        weights(0)
        load_ours.wait()

        a, b = Flat(0), Flat(1)
        if me == 0:
            c, e = Deep(2), Deep(3)
            settle(0)
            c.step(0, (1,))
            settle(1)
            a.one.far()
            settle(2)
            c.step(0, (-1,))
            settle(3)
            b.one.far()
            settle(4)
            e.step(0, (1,))
            settle(5)
            e.step(0, (-1,))
            settle(6)
            settle(7)
            c.step(1)
            settle(8)
            settle(9)
            a.one.near()
            c.step(2)
            settle(10)
            settle(11)
            e.step(1)
            settle(12)
            settle(13)
            b.one.near()
            e.step(2)
            a.one.relay()
            settle(14)
            settle(15)
            b.one.relay()
            weights(1)
            for i in (3, 4):
                c.step(i)
                e.step(i)
            for i in (5, 6):
                c.step(i)
                e.step(i)
            a.end_one()
            b.end_one()
            c.end_one()
            e.end_one()
            weights(2)
            a.two.relay()
            b.two.relay()
            c.two.relay()
            e.two.relay()
            a.end_two()
            b.end_two()
            a.relay_z()
            b.relay_z()
            c.end_two()
            e.end_two()
        else:
            d, f = Flat(2), Flat(3)
            settle(0)
            a.one.far()
            settle(1)
            b.one.far()
            settle(2)
            settle(3)
            a.one.near()
            settle(4)
            settle(5)
            b.one.near()
            for n in range(6, 10):
                settle(n)
            d.one.far()
            d.one.near()
            for n in range(10, 12):
                settle(n)
            f.one.far()
            f.one.near()
            a.one.relay()
            b.one.relay()
            for n in range(12, 16):
                settle(n)
            weights(1)
            d.one.relay()
            f.one.relay()
            a.end_one()
            b.end_one()
            weights(2)
            d.end_one()
            f.end_one()
            a.two.relay()
            b.two.relay()
            d.two.relay()
            f.two.relay()
            a.end_two()
            b.end_two()
            d.end_two()
            f.end_two()
            a.relay_z()
            b.relay_z()
            d.relay_z()
            f.relay_z()
        a.end()
        b.end()
        first_swap = swap(fin.at[me, pl.ds(0, 2)], fin.at[me, pl.ds(0, 2)], 17)
        first_swap.start()
        copy_to(partner, give, give, swap_send.at[0], swap_recv.at[0]).wait_send()
        swap_weight.wait_send()
        weights(3)
        for unit in ((c, e) if me == 0 else (d, f)):
            unit.end()
        last_swap = swap(fin.at[me, pl.ds(2, 2)], fin.at[me, pl.ds(2, 2)], 18)
        last_swap.start()
        for group in groups:
            group.drain()
        assert len(groups) <= N_SEND and len(recvs) <= N_RECV
        for i in (17, 18):
            theirs_fin = fin.at[1 - me, pl.ds(2 * (i - 17), 2)]
            swap(theirs_fin, theirs_fin, i).wait_recv()
        total = wt[5]
        for odd in (0, 1):
            @pl.when(lax.rem(zl, 2) == odd)
            def _():
                low = 4 * odd + 14 * me
                for p in (0, 1):
                    for unit in range(4):
                        out[:, p, unit * 128:(unit + 1) * 128] = fin[p, unit, low:low + 14] / total[:1]
        first_swap.wait_send()
        last_swap.wait_send()

    for me in (0, 1):
        @pl.when(core == me)
        def _():
            program(me)


def merge(deltas, ages, table):
    vmem = lambda *shape: pltpu.VMEM(shape, F32)
    return pl.pallas_call(
        kernel,
        out_shape=pltpu.VMEM((14, 2, 512), F32),
        in_specs=[
            pl.BlockSpec(memory_space=pltpu.HBM),
            pl.BlockSpec(memory_space=pltpu.HBM),
            pl.BlockSpec(memory_space=pltpu.HBM),
        ],
        out_specs=pl.BlockSpec(memory_space=pltpu.VMEM),
        scratch_shapes=[
            pltpu.SMEM((1, 1), jnp.int32),
            pltpu.SMEM((8,), F32),
            pltpu.VMEM((3584, 512), jnp.bfloat16),
            pltpu.VMEM((3584, 512), jnp.bfloat16),
            vmem(4, 32, BLOCK, 128),
            vmem(4, 32, BLOCK, 128),
            vmem(4, 32, BLOCK, 128),
            vmem(4, 3, 2, 4, BLOCK, 128),
            vmem(4, 3, 2, BLOCK, 128),
            vmem(2, 2, 7, 8, WIN, 128),
            vmem(2, 3, 2, 2, WIN, 128),
            vmem(4, 7, WIN, 128),
            vmem(4, 2, 4, BLOCK, 128),
            vmem(2, 16, WIN, 128),
            vmem(4, 2, BLOCK, 128),
            vmem(2, 7, WIN, 128),
            vmem(2, 4, WIN, 128),
            vmem(6, 8, 128),
            vmem(13, 8, 128),
            pltpu.SemaphoreType.DMA((N_SEND,)),
            pltpu.SemaphoreType.DMA((N_RECV,)),
            pltpu.SemaphoreType.DMA((4,)),
            pltpu.SemaphoreType.DMA((19,)),
            pltpu.SemaphoreType.DMA((7,)),
        ],
        compiler_params=pltpu.CompilerParams(
            collective_id=0, has_side_effects=True, vmem_limit_bytes=60 * 2**20),
        name="merge",
    )(deltas, ages, table)


def local(deltas, ages, table, params, momentum):
    merged = jnp.transpose(merge(deltas, ages, table), (1, 0, 2))
    new_momentum = momentum_decay * momentum + merged
    new_params = params - outer_rate * (merged + momentum_decay * new_momentum)
    return (new_params, new_momentum)


def solution(mesh):
    torus = Mesh(mesh.devices.reshape(2, 4, 4, 4, 2), ROW_COL)
    in_specs = (
        P(ROW_COL, None, None, None),
        P(ROW, COL),
        P(),
        P(None, ROW_COL, None),
        P(None, ROW_COL, None),
    )
    out_specs = (P(None, ROW_COL, None), P(None, ROW_COL, None))
    return jax.shard_map(local, mesh=torus, in_specs=in_specs, out_specs=out_specs, check_vma=False)
```

time: 392 us -> 56.7 us (0.14)
  waiting for transfers between devices: 287 us -> 0 us
  Pallas kernels: 0 us -> 54.5 us
  blocking collectives: 49.7 us -> 0 us
  local copies, waits for them, and re-layouts: 25.3 us -> 0.01 us
  between operations: 16 us -> 1.33 us
  other arithmetic: 13.2 us -> 0.72 us
    unnamed x2 -> x0, waiting for transfers between devices: 287 us -> none
    pallas_call x0 -> x1, Pallas kernels: none -> 54.5 us  [merge(): pl.pallas_call(kernel, out_shape=pltpu.VMEM((14, 2, 512), F32), in_specs=...]
    psum x5 -> x0, blocking collectives: 49.7 us -> none  [one_axis_at_a_time(): return functools.reduce(lax.psum, axes, value)]
    mul x1 -> x0, local copies, waits for them, and re-layouts: 25.3 us -> none  [local(): term = deltas[0].astype(jnp.float32) * factor]
    mul x1 -> x0, other arithmetic: 10.4 us -> none  [local(): term = deltas[0].astype(jnp.float32) * factor]
  transfers between devices with their start and end apart: 1 -> 0, of which waited for: 1 -> 0; matrix products, arithmetic and copies ran while one was open for 0% -> 0% of each run, Pallas kernels for 0% -> 0%
where the time goes in v2:
time: 56.7 us; the launch traced here: 56.6 us
  Pallas kernels  54.5 us (96%)
  between operations  1.33 us (2%)
  other arithmetic  0.72 us (1%)
    pallas_call x1, Pallas kernels, merge(): pl.pallas_call(kernel, out_shape=pltpu.VMEM((14, 2, 512), F32), in_specs=...  54.5 us

profile of v2, /device:TPU:1, one launch (start us, length us, event | category | flops | bytes accessed | tf_op | source)
XLA Modules:
  0.0 56.6 jit_solution(1802947282712723665)
XLA Ops:
  0.6 0.0 copy-start.1
  0.6 0.0 copy-start
  1.3 54.5 %merge.1 = f32[14,2,512]{2,1,0:T(2,128)S(1)} custom-call(bf16[1,2,3584,512]{3,2,1,0:T(8,128)(2,1)} %delta.1, s32[1,1]{1,0:T(1,128)S(6)} %copy.7.ages, f32[8]{0:T(128)} %table.1), custom_call_target="tpu_custom_call" | custom-call | tf_op jit(solution)/shard_map/merge/pallas_call | solution.py:461
  55.9 0.0 copy-done.1
  55.9 0.0 copy-done
  55.9 0.7 %fusion.1 = (f32[2,14,512]{2,0,1:T(2,128)}, f32[2,14,512]{2,0,1:T(2,128)}) fusion(f32[2,14,512]{2,0,1:T(2,128)S(1)} %copy-done, f32[14,2,512]{2,1,0:T(2,128)S(1)} %merge.1, f32[2,14,512]{2,0,1:T(2,128)S(1)} %copy-done.1), kind=kLoop, calls=%fused_computation.3 | loop fusion | flops 86016 | bytes 286720 | tf_op jit(solution)/shard_map/sub | solution.py:505
Async XLA Ops:
  0.6 55.2 %copy-start.1 = (f32[2,14,512]{2,0,1:T(2,128)S(1)}, f32[2,14,512]{2,0,1:T(2,128)}, u32[]{:S(2)}) copy-start(f32[2,14,512]{2,0,1:T(2,128)} %param.9) | copy-start | bytes 172036
  0.6 55.2 %copy-start = (f32[2,14,512]{2,0,1:T(2,128)S(1)}, f32[2,14,512]{2,0,1:T(2,128)}, u32[]{:S(2)}) copy-start(f32[2,14,512]{2,0,1:T(2,128)} %param.8) | copy-start | bytes 172036

commit v3 on v2

--- a/solution.py
+++ b/solution.py
@@ -17,15 +17,15 @@
 
 BLOCK = 112
 WIN = 32
-N_SEND, N_RECV = 13, 55
+N_SEND, N_RECV = 13, 76
 X, Y, ZX, ZY = "X", "Y", "ZX", "ZY"
-KINDS = ((X, Y, ZX, ZY), (X, Y, X, Y))
+KINDS = ((X, Y, X, Y), (X, Y, ZX, ZY))
 
 ORDERS = (
-    ((2, 1, 0), (0, 2), (2, 1, 1), (1, 2), (3, 1, 0), (3, 1, 1), (2, 0, 0), (2, 0, 1),
-     (0, 1), (0, -1), (3, 0, 0), (3, 0, 1), (1, 1), (1, -1), (0, 0), (1, 0)),
     ((0, 2), (1, 2), (0, 1), (0, -1), (1, 1), (1, -1), (2, 2), (3, 2),
      (2, 1), (2, -1), (3, 1), (3, -1), (0, 0), (1, 0), (2, 0), (3, 0)),
+    ((2, 1, 0), (2, 1, 1), (3, 1, 0), (3, 1, 1), (2, 0, 0), (2, 0, 1), (3, 0, 0), (3, 0, 1),
+     (0, 2), (1, 2), (0, 1), (0, -1), (1, 1), (1, -1), (0, 0), (1, 0)),
 )
 AHEAD = 4
 
@@ -34,8 +34,8 @@
     return lax.rem(value + 4, 4)
 
 
-def kernel(delta, ages, table, out, age, levels, theirs, ours, give, got, mine, t1, t2, tc, u2, zr,
-           g1, g1c, g2, g2c, fin, wt, wx, send_sems, recv_sems, swap_send, swap_recv, load_sems):
+def kernel(delta, ages, table, out, age, levels, theirs, ours, give, got, mine, t1, t2, tc, tz, u2, zr,
+           g1, g1c, g2, g2c, g2m, fin, wt, wx, send_sems, recv_sems, swap_send, swap_recv, load_sems):
     zh, y, x, zl, core = [lax.axis_index(name) for name in ROW_COL]
     z = zh * 4 + zl
     barrier = pltpu.get_barrier_semaphore()
@@ -71,12 +71,12 @@
         partner = (zh, y, x, zl, 1 - me)
         peers = [partner]
         peers += [at_axis(axis, s) for axis in (X, Y) for s in (1, 2, 3)]
-        peers += [at_z(z + s) for s in range(1, 8)]
+        peers += [at_z(z + s) for s in (1, -1, 2, -2)]
         for peer in peers:
             pl.semaphore_signal(barrier, inc=1, device_id=peer, device_id_type=MESH)
         load_age.wait()
         load_levels.wait()
-        weight = levels[age[0, 0]]
+        weight = levels[age[0]]
         wt[0] = jnp.full((8, 128), weight, F32)
 
         def copy_to(device, src, dst, send_sem, recv_sem):
@@ -192,21 +192,48 @@
             low = lax.rem(there, 4)
             return there // 4, pl.multiple_of((low // 2) * 56 + lax.rem(low, 2) * 24, 8)
 
+        class Quarters(Tree):
+            def __init__(self, piece, slots, axis):
+                super().__init__(piece, slots, axis)
+                self.beside = position(cross(axis))
+                self.parts = {step: new_recv() for step in (2, 1, -1, 0)}
+
+            def relay(self):
+                for s in (1, -1):
+                    k = int(s < 0)
+                    self.m0[s].wait_recv()
+                    held = self.slots.at[0, k]
+                    held[...] = held[...] + self.piece(k, wrap4(self.at + s))[...]
+                    for step, sem in self.parts.items():
+                        j = wrap4(self.beside + step)
+                        self.group.send(held.at[j], self.slots.at[2, k, j], at_axis(self.axis, s), sem)
+
+            def part(self, step, put):
+                if step == 2:
+                    arrived(self.slots.at[1], self.rest)
+                j = wrap4(self.beside + step)
+                arrived(self.slots.at[2, :, j], self.parts[step])
+                for h in (0, 1):
+                    put(h, j, self.piece(h, self.at)[j] + self.slots[2, h, j] + self.slots[1, 1 - h, j])
+
         class Flat:
             def __init__(self, unit):
                 axis = kinds[unit]
                 self.unit = unit
-                self.one = Tree(lambda h, d: mine.at[unit, pl.ds(d * 8 + h * 4, 4)], t1.at[unit], axis)
+                self.one = Quarters(lambda h, d: mine.at[unit, pl.ds(d * 8 + h * 4, 4)], t1.at[unit], axis)
                 self.two = Tree(lambda h, d: g1.at[unit, h, d], t2.at[unit], cross(axis))
                 self.group, self.last, self.far_sem = Group(zr.at[unit]), new_recv(), new_recv()
                 self.way = 1 if unit % 2 == 0 else -1
 
-            def end_one(self):
-                def put(h, value):
-                    g1[self.unit, h] = value
-                self.one.finish(put)
-                self.two.far()
-                self.two.near()
+            def part(self, n):
+                def put(h, j, value):
+                    g1[self.unit, h, j] = value
+                for step in ((2,), (1, -1), (0,))[n]:
+                    self.one.part(step, put)
+                if n == 0:
+                    self.two.far()
+                elif n == 1:
+                    self.two.near()
 
             def end_two(self):
                 def put(h, value):
@@ -242,19 +269,12 @@
                     value = value + zr[self.unit, n]
                 fin[me, self.unit] = value
 
-        class Deep:
+        class Ring:
             dist = (4, 3, 3, 2, 2, 1, 1)
 
-            def __init__(self, unit):
-                self.unit, self.n = unit, unit - 2
-                self.axis = X if kinds[unit] == ZX else Y
-                self.copies, self.ring = {}, Group(tc.at[self.n])
-                self.two = Tree(lambda h, d: g1c.at[self.n, pl.ds(d * 4 + h * 2, 2)], u2.at[self.n], self.axis)
-                self.group, self.last = Group(g2c.at[self.n, pl.ds(4, 3)]), new_recv()
-
-            def piece(self, there, half):
-                up, start = window(there)
-                return mine.at[self.unit, pl.ds(up * 16 + half * 8, 8), pl.ds(start, WIN)]
+            def __init__(self, piece, slots):
+                self.piece, self.slots = piece, slots
+                self.group, self.copies = Group(slots), {}
 
             def step(self, i, ways=(1, -1)):
                 for s in ways:
@@ -262,54 +282,106 @@
                     piece = self.piece(z + s * self.dist[i], k if i % 2 == 0 else 1 - k)
                     if i >= 2:
                         self.copies[s, i - 2].wait_recv()
-                        held = tc.at[self.n, k, i - 2]
+                        held = self.slots.at[k, i - 2]
                         held[...] = held[...] + piece[...]
                         piece = held
-                    self.copies[s, i] = self.ring.send(piece, tc.at[self.n, k, i], at_z(z + s), new_recv())
-
-            def end_one(self):
+                    self.copies[s, i] = self.group.send(piece, self.slots.at[k, i], at_z(z + s), new_recv())
+
+            def finish(self, put):
                 for i in (5, 6):
                     for s in (1, -1):
                         self.copies[s, i].wait_recv()
                 for half in (0, 1):
-                    g1c[self.n, half * 8:half * 8 + 8] = (
-                        self.piece(z, half)[...] + tc[self.n, half, 6] + tc[self.n, 1 - half, 5])
-                self.two.far()
-                self.two.near()
+                    put(half, self.piece(z, half)[...] + self.slots[half, 6] + self.slots[1 - half, 5])
+
+        class Direct:
+            def __init__(self, held, axis, unit):
+                self.held, self.axis, self.unit = held, axis, unit
+                self.group, self.sem = Group(held.at[pl.ds(4, 3)]), new_recv()
+
+            def start(self):
+                for s in (2, 1, 3):
+                    src = self.held.at[wrap4(position(self.axis) + s)]
+                    self.group.send(src, self.held.at[3 + s], at_axis(self.axis, s), self.sem)
+
+            def end(self):
+                arrived(self.held.at[pl.ds(4, 3)], self.sem)
+                own = self.held[position(self.axis)]
+                fin[me, self.unit] = own + (self.held[4] + self.held[5] + self.held[6])
+
+        class Deep:
+            def __init__(self, unit):
+                n = unit - 2
+                axis = X if kinds[unit] == ZX else Y
+
+                def piece(there, half):
+                    up, start = window(there)
+                    return mine.at[unit, pl.ds(up * 16 + half * 8, 8), pl.ds(start, WIN)]
+
+                self.n, self.one = n, Ring(piece, tc.at[n])
+                self.two = Tree(lambda h, d: g1c.at[n, pl.ds(d * 4 + h * 2, 2)], u2.at[n], axis)
+                self.last = Direct(g2c.at[n], cross(axis), unit)
+                self.step, self.end = self.one.step, self.last.end
+
+            def end_one(self):
+                def put(half, value):
+                    g1c[self.n, half * 8:half * 8 + 8] = value
+                self.one.finish(put)
 
             def end_two(self):
                 def put(h, value):
                     g2c[self.n, h * 2:h * 2 + 2] = value
                 self.two.finish(put)
-                axis = cross(self.axis)
-                for s in (2, 1, 3):
-                    src = g2c.at[self.n, wrap4(position(axis) + s)]
-                    self.group.send(src, g2c.at[self.n, 3 + s], at_axis(axis, s), self.last)
-
-            def end(self):
-                arrived(g2c.at[self.n, pl.ds(4, 3)], self.last)
-                fin[me, self.unit] = g2c[self.n, position(cross(self.axis))] + (
-                    g2c[self.n, 4] + g2c[self.n, 5] + g2c[self.n, 6])
-
-        weight_group, weight_sems = Group(wx), [new_recv() for _ in range(3)]
+                self.last.start()
+
+        class Mixed:
+            def __init__(self, unit):
+                axis = kinds[unit]
+
+                def piece(there, half):
+                    up, start = window(there)
+                    return g1.at[unit, up, pl.ds(half * 2, 2), pl.ds(start, WIN)]
+
+                self.unit = unit
+                self.one = Tree(lambda h, d: mine.at[unit, pl.ds(d * 8 + h * 4, 4)], t1.at[unit], axis)
+                self.two = Ring(piece, tz.at[unit])
+                self.last = Direct(g2m.at[unit], cross(axis), unit)
+                self.step, self.end = self.two.step, self.last.end
+
+            def end_one(self):
+                def put(h, value):
+                    g1[self.unit, h] = value
+                self.one.finish(put)
+
+            def end_two(self):
+                def put(half, value):
+                    g2m[self.unit, half * 2:half * 2 + 2] = value
+                self.two.finish(put)
+                self.last.start()
+
+        weight_group, weight_sems = Group(wx), [new_recv() for _ in range(4)]
+
+        def spread(value, slots, devices, stage):
+            wt[2 + stage] = value
+            for slot, device in zip(slots, devices):
+                weight_group.send(wt.at[2 + stage], wx.at[slot], device, weight_sems[stage])
 
         def weights(stage):
-            spans = ((), (1, 2, 3), (1, 2, 3), (4, 3, 5, 2, 6, 1, 7))
-            lows = (0, 3, 6)
             if stage == 0:
                 swap(wt.at[1], wt.at[1], 16).wait_recv()
-                wt[2] = wt[0] + wt[1]
+                return spread(wt[0] + wt[1], (0, 1, 2), [at_axis(X, s) for s in (1, 2, 3)], 0)
+            low, count = ((0, 3), (3, 3), (6, 4), (10, 2))[stage - 1]
+            arrived(wx.at[pl.ds(low, count)], weight_sems[stage - 1])
+            if stage == 1:
+                spread(wt[2] + wx[0] + wx[1] + wx[2], (3, 4, 5), [at_axis(Y, s) for s in (1, 2, 3)], 1)
+            elif stage == 2:
+                spread(wt[3] + wx[3] + wx[4] + wx[5], (6, 7, 8, 9), [at_z(z + s) for s in (-1, 1, -2, 2)], 2)
+            elif stage == 3:
+                wt[5] = wx[6] + wx[8]
+                weight_group.send(wt.at[5], wx.at[10], at_z(z - 2), weight_sems[3])
+                weight_group.send(wx.at[7], wx.at[11], at_z(z + 2), weight_sems[3])
             else:
-                low, count = lows[stage - 1], len(spans[stage])
-                arrived(wx.at[pl.ds(low, count)], weight_sems[stage - 1])
-                value = wt[1 + stage]
-                for n in range(count):
-                    value = value + wx[low + n]
-                wt[2 + stage] = value
-            if stage < 3:
-                for n, s in enumerate(spans[stage + 1]):
-                    device = at_z(z + s) if stage == 2 else at_axis((X, Y)[stage], s)
-                    weight_group.send(wt.at[2 + stage], wx.at[lows[stage] + n], device, weight_sems[stage])
+                wt[6] = wt[4] + (wx[6] + wx[7] + wx[8] + wx[9]) + (wx[10] + wx[11])
 
         put_together(0)
         load_ours.start()
@@ -323,63 +395,14 @@
         weights(0)
         load_ours.wait()
 
-        a, b = Flat(0), Flat(1)
+        def hand_over(low, i):
+            part = fin.at[me, pl.ds(low, 2)]
+            copy = swap(part, part, i)
+            copy.start()
+            return copy
+
         if me == 0:
-            c, e = Deep(2), Deep(3)
-            settle(0)
-            c.step(0, (1,))
-            settle(1)
-            a.one.far()
-            settle(2)
-            c.step(0, (-1,))
-            settle(3)
-            b.one.far()
-            settle(4)
-            e.step(0, (1,))
-            settle(5)
-            e.step(0, (-1,))
-            settle(6)
-            settle(7)
-            c.step(1)
-            settle(8)
-            settle(9)
-            a.one.near()
-            c.step(2)
-            settle(10)
-            settle(11)
-            e.step(1)
-            settle(12)
-            settle(13)
-            b.one.near()
-            e.step(2)
-            a.one.relay()
-            settle(14)
-            settle(15)
-            b.one.relay()
-            weights(1)
-            for i in (3, 4):
-                c.step(i)
-                e.step(i)
-            for i in (5, 6):
-                c.step(i)
-                e.step(i)
-            a.end_one()
-            b.end_one()
-            c.end_one()
-            e.end_one()
-            weights(2)
-            a.two.relay()
-            b.two.relay()
-            c.two.relay()
-            e.two.relay()
-            a.end_two()
-            b.end_two()
-            a.relay_z()
-            b.relay_z()
-            c.end_two()
-            e.end_two()
-        else:
-            d, f = Flat(2), Flat(3)
+            a, b, d, f = Mixed(0), Mixed(1), Flat(2), Flat(3)
             settle(0)
             a.one.far()
             settle(1)
@@ -390,56 +413,144 @@
             settle(4)
             settle(5)
             b.one.near()
-            for n in range(6, 10):
-                settle(n)
+            settle(6)
+            settle(7)
+            settle(8)
+            settle(9)
+            weights(1)
+            a.one.relay()
             d.one.far()
             d.one.near()
-            for n in range(10, 12):
-                settle(n)
+            b.one.relay()
             f.one.far()
+            settle(10)
+            settle(11)
             f.one.near()
+            settle(12)
+            settle(13)
+            settle(14)
+            settle(15)
+            a.end_one()
+            a.step(0)
+            a.step(1)
+            b.end_one()
+            b.step(0)
+            b.step(1)
+            d.one.relay()
+            f.one.relay()
+            weights(2)
+            a.step(2)
+            a.step(3)
+            b.step(2)
+            b.step(3)
+            a.step(4)
+            a.step(5)
+            b.step(4)
+            b.step(5)
+            weights(3)
+            d.part(0)
+            f.part(0)
+            a.step(6)
+            b.step(6)
+            d.part(1)
+            f.part(1)
+            d.part(2)
+            f.part(2)
+            d.two.relay()
+            f.two.relay()
+            d.end_two()
+            f.end_two()
+            a.end_two()
+            b.end_two()
+            d.relay_z()
+            f.relay_z()
+            a.end()
+            b.end()
+            first_swap = hand_over(0, 17)
+            d.end()
+            f.end()
+            last_swap = hand_over(2, 18)
+        else:
+            a, b, c, e = Flat(0), Flat(1), Deep(2), Deep(3)
+            settle(0)
+            c.step(0, (1,))
+            settle(1)
+            c.step(0, (-1,))
+            settle(2)
+            e.step(0, (1,))
+            settle(3)
+            e.step(0, (-1,))
+            settle(4)
+            settle(5)
+            c.step(1)
+            c.step(2)
+            settle(6)
+            settle(7)
+            e.step(1)
+            e.step(2)
+            weights(1)
+            settle(8)
+            settle(9)
+            c.step(3)
+            settle(10)
+            settle(11)
+            settle(12)
+            c.step(4)
+            settle(13)
+            settle(14)
+            e.step(3)
+            settle(15)
+            e.step(4)
+            c.step(5)
+            a.one.far()
+            b.one.far()
+            a.one.near()
+            b.one.near()
+            e.step(5)
+            c.step(6)
             a.one.relay()
             b.one.relay()
-            for n in range(12, 16):
-                settle(n)
-            weights(1)
-            d.one.relay()
-            f.one.relay()
-            a.end_one()
-            b.end_one()
+            e.step(6)
             weights(2)
-            d.end_one()
-            f.end_one()
+            a.part(0)
+            b.part(0)
+            a.part(1)
+            b.part(1)
+            a.part(2)
+            b.part(2)
+            c.end_one()
+            c.two.far()
+            c.two.near()
             a.two.relay()
             b.two.relay()
-            d.two.relay()
-            f.two.relay()
+            weights(3)
+            e.end_one()
+            e.two.far()
+            e.two.near()
             a.end_two()
             b.end_two()
-            d.end_two()
-            f.end_two()
+            c.two.relay()
+            e.two.relay()
             a.relay_z()
             b.relay_z()
-            d.relay_z()
-            f.relay_z()
-        a.end()
-        b.end()
-        first_swap = swap(fin.at[me, pl.ds(0, 2)], fin.at[me, pl.ds(0, 2)], 17)
-        first_swap.start()
+            c.end_two()
+            e.end_two()
+            a.end()
+            b.end()
+            first_swap = hand_over(0, 17)
+            c.end()
+            e.end()
+            last_swap = hand_over(2, 18)
         copy_to(partner, give, give, swap_send.at[0], swap_recv.at[0]).wait_send()
         swap_weight.wait_send()
-        weights(3)
-        for unit in ((c, e) if me == 0 else (d, f)):
-            unit.end()
-        last_swap = swap(fin.at[me, pl.ds(2, 2)], fin.at[me, pl.ds(2, 2)], 18)
-        last_swap.start()
+        weights(4)
         for group in groups:
             group.drain()
         assert len(groups) <= N_SEND and len(recvs) <= N_RECV
         for i in (17, 18):
             theirs_fin = fin.at[1 - me, pl.ds(2 * (i - 17), 2)]
             swap(theirs_fin, theirs_fin, i).wait_recv()
-        total = wt[5]
+        total = wt[6]
         for odd in (0, 1):
             @pl.when(lax.rem(zl, 2) == odd)
             def _():
@@ -468,7 +579,7 @@
         ],
         out_specs=pl.BlockSpec(memory_space=pltpu.VMEM),
         scratch_shapes=[
-            pltpu.SMEM((1, 1), jnp.int32),
+            pltpu.SMEM((1,), jnp.int32),
             pltpu.SMEM((8,), F32),
             pltpu.VMEM((3584, 512), jnp.bfloat16),
             pltpu.VMEM((3584, 512), jnp.bfloat16),
@@ -478,15 +589,17 @@
             vmem(4, 3, 2, 4, BLOCK, 128),
             vmem(4, 3, 2, BLOCK, 128),
             vmem(2, 2, 7, 8, WIN, 128),
+            vmem(2, 2, 7, 2, WIN, 128),
             vmem(2, 3, 2, 2, WIN, 128),
             vmem(4, 7, WIN, 128),
             vmem(4, 2, 4, BLOCK, 128),
             vmem(2, 16, WIN, 128),
             vmem(4, 2, BLOCK, 128),
             vmem(2, 7, WIN, 128),
+            vmem(2, 7, WIN, 128),
             vmem(2, 4, WIN, 128),
-            vmem(6, 8, 128),
-            vmem(13, 8, 128),
+            vmem(7, 8, 128),
+            vmem(12, 8, 128),
             pltpu.SemaphoreType.DMA((N_SEND,)),
             pltpu.SemaphoreType.DMA((N_RECV,)),
             pltpu.SemaphoreType.DMA((4,)),
@@ -496,7 +609,7 @@
         compiler_params=pltpu.CompilerParams(
             collective_id=0, has_side_effects=True, vmem_limit_bytes=60 * 2**20),
         name="merge",
-    )(deltas, ages, table)
+    )(deltas, ages.reshape(1), table)
 
 
 def local(deltas, ages, table, params, momentum):

time: 56.7 us -> 53.8 us (0.949)
  Pallas kernels: 54.5 us -> 51.6 us
    pallas_call x1, Pallas kernels: 54.5 us -> 51.6 us  [merge(): pl.pallas_call(kernel, out_shape=pltpu.VMEM((14, 2, 512), F32), in_specs=...]
where the time goes in v3:
time: 53.8 us; the launch traced here: 53.7 us
  Pallas kernels  51.6 us (96%)
  between operations  1.33 us (2%)
  other arithmetic  0.72 us (1%)
    pallas_call x1, Pallas kernels, merge(): pl.pallas_call(kernel, out_shape=pltpu.VMEM((14, 2, 512), F32), in_specs=...  51.6 us

profile of v3, /device:TPU:1, one launch (start us, length us, event | category | flops | bytes accessed | tf_op | source)
XLA Modules:
  0.0 53.7 jit_solution(15243691889377178265)
XLA Ops:
  0.6 0.0 copy-start.1
  0.6 0.0 copy-start
  1.3 51.6 %merge.1 = f32[14,2,512]{2,1,0:T(2,128)S(1)} custom-call(bf16[1,2,3584,512]{3,2,1,0:T(8,128)(2,1)} %delta.1, s32[1]{0:T(128)} %bitcast.9.ages, f32[8]{0:T(128)} %table.1), custom_call_target="tpu_custom_call" | custom-call | tf_op jit(solution)/shard_map/merge/pallas_call | solution.py:572
  53.0 0.0 copy-done.1
  53.0 0.0 copy-done
  53.0 0.7 %fusion.1 = (f32[2,14,512]{2,0,1:T(2,128)}, f32[2,14,512]{2,0,1:T(2,128)}) fusion(f32[2,14,512]{2,0,1:T(2,128)S(1)} %copy-done, f32[14,2,512]{2,1,0:T(2,128)S(1)} %merge.1, f32[2,14,512]{2,0,1:T(2,128)S(1)} %copy-done.1), kind=kLoop, calls=%fused_computation.3 | loop fusion | flops 86016 | bytes 286720 | tf_op jit(solution)/shard_map/sub | solution.py:618
Async XLA Ops:
  0.6 52.3 %copy-start.1 = (f32[2,14,512]{2,0,1:T(2,128)S(1)}, f32[2,14,512]{2,0,1:T(2,128)}, u32[]{:S(2)}) copy-start(f32[2,14,512]{2,0,1:T(2,128)} %param.9) | copy-start | bytes 172036
  0.6 52.3 %copy-start = (f32[2,14,512]{2,0,1:T(2,128)S(1)}, f32[2,14,512]{2,0,1:T(2,128)}, u32[]{:S(2)}) copy-start(f32[2,14,512]{2,0,1:T(2,128)} %param.8) | copy-start | bytes 172036

commit v4 on v3

--- a/solution.py
+++ b/solution.py
@@ -17,7 +17,7 @@
 
 BLOCK = 112
 WIN = 32
-N_SEND, N_RECV = 13, 76
+N_SEND, N_RECV = 13, 44
 X, Y, ZX, ZY = "X", "Y", "ZX", "ZY"
 KINDS = ((X, Y, X, Y), (X, Y, ZX, ZY))
 
@@ -145,6 +145,9 @@
             gifts.append(swap(give.at[unit, pl.ds(base, 8)], got.at[unit, pl.ds(base, 8)], n))
 
         def settle(n):
+            if n + AHEAD < 16:
+                put_together(n + AHEAD)
+                gifts[-1].start()
             unit, *step = order[n]
             kind = kinds[unit]
             base = chunk(kind, step)
@@ -154,21 +157,17 @@
             def _(k):
                 mine[unit, base + k] = got[unit, base + k] + term(ours, unit, kind, base + k)
 
-            if n + AHEAD < 16:
-                put_together(n + AHEAD)
-                gifts[-1].start()
-
         class Tree:
             def __init__(self, piece, slots, axis):
                 self.piece, self.slots, self.axis, self.at = piece, slots, axis, position(axis)
                 self.group = Group(slots)
-                self.m0, self.first, self.rest = {}, {1: new_recv(), -1: new_recv()}, new_recv()
+                self.first, self.rest = new_recv(), new_recv()
 
             def far(self):
                 for s in (1, -1):
                     src = self.piece(int(s < 0), wrap4(self.at + 2))
                     dst = self.slots.at[0, int(s < 0)]
-                    self.m0[s] = self.group.send(src, dst, at_axis(self.axis, s), self.first[s])
+                    self.group.send(src, dst, at_axis(self.axis, s), self.first)
 
             def near(self):
                 for s in (1, -1):
@@ -176,8 +175,8 @@
                     self.group.send(src, self.slots.at[1, int(s < 0)], at_axis(self.axis, s), self.rest)
 
             def relay(self):
+                arrived(self.slots.at[0], self.first)
                 for s in (1, -1):
-                    self.m0[s].wait_recv()
                     held = self.slots.at[0, int(s < 0)]
                     held[...] = held[...] + self.piece(int(s < 0), wrap4(self.at + s))[...]
                     self.group.send(held, self.slots.at[2, int(s < 0)], at_axis(self.axis, s), self.rest)
@@ -199,9 +198,9 @@
                 self.parts = {step: new_recv() for step in (2, 1, -1, 0)}
 
             def relay(self):
+                arrived(self.slots.at[0], self.first)
                 for s in (1, -1):
                     k = int(s < 0)
-                    self.m0[s].wait_recv()
                     held = self.slots.at[0, k]
                     held[...] = held[...] + self.piece(k, wrap4(self.at + s))[...]
                     for step, sem in self.parts.items():
@@ -274,23 +273,23 @@
 
             def __init__(self, piece, slots):
                 self.piece, self.slots = piece, slots
-                self.group, self.copies = Group(slots), {}
+                self.group, self.sems = Group(slots), [new_recv() for _ in self.dist]
 
             def step(self, i, ways=(1, -1)):
+                if i >= 2:
+                    arrived(self.slots.at[:, i - 2], self.sems[i - 2])
                 for s in ways:
                     k = int(s < 0)
                     piece = self.piece(z + s * self.dist[i], k if i % 2 == 0 else 1 - k)
                     if i >= 2:
-                        self.copies[s, i - 2].wait_recv()
                         held = self.slots.at[k, i - 2]
                         held[...] = held[...] + piece[...]
                         piece = held
-                    self.copies[s, i] = self.group.send(piece, self.slots.at[k, i], at_z(z + s), new_recv())
+                    self.group.send(piece, self.slots.at[k, i], at_z(z + s), self.sems[i])
 
             def finish(self, put):
                 for i in (5, 6):
-                    for s in (1, -1):
-                        self.copies[s, i].wait_recv()
+                    arrived(self.slots.at[:, i], self.sems[i])
                 for half in (0, 1):
                     put(half, self.piece(z, half)[...] + self.slots[half, 6] + self.slots[1 - half, 5])
 
@@ -438,7 +437,6 @@
             b.step(1)
             d.one.relay()
             f.one.relay()
-            weights(2)
             a.step(2)
             a.step(3)
             b.step(2)
@@ -447,19 +445,20 @@
             a.step(5)
             b.step(4)
             b.step(5)
-            weights(3)
+            weights(2)
             d.part(0)
             f.part(0)
-            a.step(6)
-            b.step(6)
             d.part(1)
             f.part(1)
             d.part(2)
             f.part(2)
+            a.step(6)
+            b.step(6)
             d.two.relay()
             f.two.relay()
             d.end_two()
             f.end_two()
+            weights(3)
             a.end_two()
             b.end_two()
             d.relay_z()
@@ -501,34 +500,34 @@
             e.step(3)
             settle(15)
             e.step(4)
-            c.step(5)
+            weights(2)
             a.one.far()
             b.one.far()
             a.one.near()
             b.one.near()
+            c.step(5)
             e.step(5)
             c.step(6)
+            e.step(6)
             a.one.relay()
             b.one.relay()
-            e.step(6)
-            weights(2)
             a.part(0)
             b.part(0)
             a.part(1)
             b.part(1)
             a.part(2)
             b.part(2)
+            a.two.relay()
+            b.two.relay()
             c.end_one()
             c.two.far()
             c.two.near()
-            a.two.relay()
-            b.two.relay()
-            weights(3)
             e.end_one()
             e.two.far()
             e.two.near()
             a.end_two()
             b.end_two()
+            weights(3)
             c.two.relay()
             e.two.relay()
             a.relay_z()
@@ -543,13 +542,13 @@
             last_swap = hand_over(2, 18)
         copy_to(partner, give, give, swap_send.at[0], swap_recv.at[0]).wait_send()
         swap_weight.wait_send()
-        weights(4)
         for group in groups:
             group.drain()
         assert len(groups) <= N_SEND and len(recvs) <= N_RECV
         for i in (17, 18):
             theirs_fin = fin.at[1 - me, pl.ds(2 * (i - 17), 2)]
             swap(theirs_fin, theirs_fin, i).wait_recv()
+        weights(4)
         total = wt[6]
         for odd in (0, 1):
             @pl.when(lax.rem(zl, 2) == odd)

time: 53.8 us -> 53.7 us (level)
  no operation moved by 1% of the time
where the time goes in v4:
time: 53.7 us; the launch traced here: 53.5 us
  Pallas kernels  51.5 us (96%)
  between operations  1.33 us (2%)
  other arithmetic  0.72 us (1%)
    pallas_call x1, Pallas kernels, merge(): pl.pallas_call(kernel, out_shape=pltpu.VMEM((14, 2, 512), F32), in_specs=...  51.5 us

profile of v4, /device:TPU:1, one launch (start us, length us, event | category | flops | bytes accessed | tf_op | source)
XLA Modules:
  0.0 53.5 jit_solution(2708686693605282251)
XLA Ops:
  0.6 0.0 copy-start.1
  0.6 0.0 copy-start
  1.3 51.5 %merge.1 = f32[14,2,512]{2,1,0:T(2,128)S(1)} custom-call(bf16[1,2,3584,512]{3,2,1,0:T(8,128)(2,1)} %delta.1, s32[1]{0:T(128)} %bitcast.9.ages, f32[8]{0:T(128)} %table.1), custom_call_target="tpu_custom_call" | custom-call | tf_op jit(solution)/shard_map/merge/pallas_call | solution.py:571
  52.8 0.0 copy-done.1
  52.8 0.0 copy-done
  52.8 0.7 %fusion.1 = (f32[2,14,512]{2,0,1:T(2,128)}, f32[2,14,512]{2,0,1:T(2,128)}) fusion(f32[2,14,512]{2,0,1:T(2,128)S(1)} %copy-done, f32[14,2,512]{2,1,0:T(2,128)S(1)} %merge.1, f32[2,14,512]{2,0,1:T(2,128)S(1)} %copy-done.1), kind=kLoop, calls=%fused_computation.3 | loop fusion | flops 86016 | bytes 286720 | tf_op jit(solution)/shard_map/sub | solution.py:617
Async XLA Ops:
  0.6 52.1 %copy-start.1 = (f32[2,14,512]{2,0,1:T(2,128)S(1)}, f32[2,14,512]{2,0,1:T(2,128)}, u32[]{:S(2)}) copy-start(f32[2,14,512]{2,0,1:T(2,128)} %param.9) | copy-start | bytes 172036
  0.6 52.1 %copy-start = (f32[2,14,512]{2,0,1:T(2,128)S(1)}, f32[2,14,512]{2,0,1:T(2,128)}, u32[]{:S(2)}) copy-start(f32[2,14,512]{2,0,1:T(2,128)} %param.8) | copy-start | bytes 172036

commit v5 on v4

--- a/solution.py
+++ b/solution.py
@@ -28,6 +28,7 @@
      (0, 2), (1, 2), (0, 1), (0, -1), (1, 1), (1, -1), (0, 0), (1, 0)),
 )
 AHEAD = 4
+STRAIGHT = ((), (1,))
 
 
 def wrap4(value):
@@ -238,6 +239,10 @@
                 def put(h, value):
                     g2[self.unit, h] = value
                 self.two.finish(put)
+                if self.unit in STRAIGHT[me]:
+                    for s in (4, 3, -3, 2, -2, 1, -1):
+                        self.send_z(s, s, (s - 1) % 8, self.last)
+                    return
                 self.send_z(4, 2 * self.way, 4, self.far_sem)
                 for s in (1, -1):
                     self.send_z(3 * s, s, 5 + int(s < 0), self.far_sem)
@@ -252,6 +257,8 @@
                 self.group.send(self.piece_z(z + there), zr.at[self.unit, slot], at_z(z + step), sem)
 
             def relay_z(self):
+                if self.unit in STRAIGHT[me]:
+                    return
                 arrived(zr.at[self.unit, pl.ds(4, 3)], self.far_sem)
                 for s in (1, -1):
                     held = zr.at[self.unit, 5 + int(s < 0)]
@@ -262,9 +269,10 @@
                     self.group.send(held, zr.at[self.unit, 2 + int(s < 0)], at_z(z + 2 * s), self.last)
 
             def end(self):
-                arrived(zr.at[self.unit, pl.ds(0, 4)], self.last)
+                count = 7 if self.unit in STRAIGHT[me] else 4
+                arrived(zr.at[self.unit, pl.ds(0, count)], self.last)
                 value = self.piece_z(z)[...]
-                for n in range(4):
+                for n in range(count):
                     value = value + zr[self.unit, n]
                 fin[me, self.unit] = value
 

time: 53.7 us -> 53.5 us (level)
  no operation moved by 1% of the time
where the time goes in v5:
time: 53.5 us; the launch traced here: 53.4 us
  Pallas kernels  51.3 us (96%)
  between operations  1.33 us (2%)
  other arithmetic  0.72 us (1%)
    pallas_call x1, Pallas kernels, merge(): pl.pallas_call(kernel, out_shape=pltpu.VMEM((14, 2, 512), F32), in_specs=...  51.3 us

profile of v5, /device:TPU:1, one launch (start us, length us, event | category | flops | bytes accessed | tf_op | source)
XLA Modules:
  0.0 53.4 jit_solution(10791384823257567573)
XLA Ops:
  0.6 0.0 copy-start.1
  0.6 0.0 copy-start
  1.3 51.3 %merge.1 = f32[14,2,512]{2,1,0:T(2,128)S(1)} custom-call(bf16[1,2,3584,512]{3,2,1,0:T(8,128)(2,1)} %delta.1, s32[1]{0:T(128)} %bitcast.9.ages, f32[8]{0:T(128)} %table.1), custom_call_target="tpu_custom_call" | custom-call | tf_op jit(solution)/shard_map/merge/pallas_call | solution.py:579
  52.6 0.0 copy-done.1
  52.6 0.0 copy-done
  52.6 0.7 %fusion.1 = (f32[2,14,512]{2,0,1:T(2,128)}, f32[2,14,512]{2,0,1:T(2,128)}) fusion(f32[2,14,512]{2,0,1:T(2,128)S(1)} %copy-done, f32[14,2,512]{2,1,0:T(2,128)S(1)} %merge.1, f32[2,14,512]{2,0,1:T(2,128)S(1)} %copy-done.1), kind=kLoop, calls=%fused_computation.3 | loop fusion | flops 86016 | bytes 286720 | tf_op jit(solution)/shard_map/sub | solution.py:625
Async XLA Ops:
  0.6 52.0 %copy-start.1 = (f32[2,14,512]{2,0,1:T(2,128)S(1)}, f32[2,14,512]{2,0,1:T(2,128)}, u32[]{:S(2)}) copy-start(f32[2,14,512]{2,0,1:T(2,128)} %param.9) | copy-start | bytes 172036
  0.6 52.0 %copy-start = (f32[2,14,512]{2,0,1:T(2,128)S(1)}, f32[2,14,512]{2,0,1:T(2,128)}, u32[]{:S(2)}) copy-start(f32[2,14,512]{2,0,1:T(2,128)} %param.8) | copy-start | bytes 172036
